TPU v7x, 32 devices: a whole 2x2x4 slice. The times are simulated.
32 devices in a mesh: rep: 2 (over x), exp: 16 (over z, y, core).
Axes of the slice: x: 2, y: 2, z: 4, core: 2. Of those that a mesh axis runs over, the one named last changes fastest.
Arguments:
- a_tokens: bfloat16 [64, 7168], P(('rep', 'exp')), parts along dimension 0, may hold values from -6 to 6
- a_gain: float32 [7168], replicated, may hold values from 0.25 to 1.75
- dense_gate: bfloat16 [7168, 18432], P(None, 'exp'), may hold values from -0.0625 to 0.0625
- dense_up: bfloat16 [7168, 18432], P(None, 'exp'), may hold values from -0.0625 to 0.0625
- dense_down: bfloat16 [18432, 7168], P('exp'), may hold values from -0.046875 to 0.046875
- b_tokens: bfloat16 [128, 7168], P(('rep', 'exp')), parts along dimension 0, may hold values from -6 to 6
- b_gain: float32 [7168], replicated, may hold values from 0.25 to 1.75
- expert_ids: int32 [128, 8], P(('rep', 'exp')), parts along dimension 0, may hold values from 0 to 15, all different within a row; in each aligned block of 4 rows (0 to 3, 4 to 7, ...) at most 3 rows name the same one
- route_weights: float32 [128, 8], P(('rep', 'exp')), parts along dimension 0, may hold values from 0.05 to 0.5
- expert_gate: bfloat16 [16, 7168, 1024], P('exp'), may hold values from -0.0625 to 0.0625
- expert_up: bfloat16 [16, 7168, 1024], P('exp'), may hold values from -0.0625 to 0.0625
- expert_down: bfloat16 [16, 1024, 7168], P('exp'), may hold values from -0.1875 to 0.1875
Outputs:
- a_out: bfloat16 [64, 7168], P(('rep', 'exp')), parts along dimension 0
- b_out: bfloat16 [128, 7168], P(('rep', 'exp')), parts along dimension 0
There are 2 independent parts, one for each index of `rep`. A program takes and returns all parts, laid end to end along the dimension named above; an argument that names none is the same for every part. Nothing has to cross between parts.
Inputs may be any that keep to these rules, and one draw needn't show every extreme that they name: `expert_ids`: each row names 8 different experts. Among the rows of one device no expert is named more than 3 times, and in some devices one expert is named exactly 3 times.
All inputs are finite; a program needn't handle non-finite values.
Results may differ from a plain program's by a relative error of at most 0.008.
Values may be sent and summed in bfloat16 or wider, within the bound.
A program may use at most 192 MiB of HBM per device.

v0:
```python
import jax
import jax.numpy as jnp
from jax import lax
from jax.sharding import PartitionSpec as P

EXPERTS = 16
CAP = 3


def normed(values, gain_vec):
    return values * lax.rsqrt(jnp.mean(values * values, axis=-1, keepdims=True) + 1e-06) * gain_vec


def shards(
    a_tokens,
    a_gain,
    dense_gate,
    dense_up,
    dense_down,
    b_tokens,
    b_gain,
    expert_ids,
    route_weights,
    expert_gate,
    expert_up,
    expert_down,
):
    devices = lax.axis_size("exp")
    group_size = devices // EXPERTS
    model_width = b_tokens.shape[1]
    a_float = a_tokens.astype(jnp.float32)
    a_normed = normed(a_float, a_gain).astype(jnp.bfloat16)
    block_rows = lax.all_gather(a_normed, "exp", axis=0, tiled=True)
    gate_proj = jnp.dot(block_rows, dense_gate, preferred_element_type=jnp.float32)
    up_proj = jnp.dot(block_rows, dense_up, preferred_element_type=jnp.float32)
    hidden = (jax.nn.silu(gate_proj) * up_proj).astype(jnp.bfloat16)
    block_rows = hidden
    a_sum = lax.psum_scatter(
        jnp.dot(block_rows, dense_down, preferred_element_type=jnp.float32),
        "exp",
        scatter_dimension=0,
        tiled=True,
    )
    a_out = (a_float + a_sum).astype(jnp.bfloat16)
    row_count = b_tokens.shape[0]
    b_float = b_tokens.astype(jnp.float32)
    b_normed = normed(b_float, b_gain).astype(jnp.bfloat16)
    onehot = (expert_ids[:, :, None] == jnp.arange(EXPERTS, dtype=jnp.int32)[None, None, :]).astype(
        jnp.float32
    )
    chosen = jnp.sum(onehot, axis=1)
    before = jnp.cumsum(chosen, axis=0) - chosen
    slot_hit = (before[:, :, None] == jnp.arange(CAP, dtype=jnp.float32)[None, None, :]).astype(
        jnp.float32
    ) * chosen[:, :, None]
    weights_te = jnp.einsum("tk,tke->te", route_weights, onehot)
    placing = slot_hit.reshape(row_count, EXPERTS * CAP)
    mixing = (weights_te[:, :, None] * slot_hit).reshape(row_count, EXPERTS * CAP)
    packed = jnp.dot(placing.T.astype(jnp.bfloat16), b_normed, preferred_element_type=jnp.float32)
    packed = packed.astype(jnp.bfloat16).reshape(EXPERTS, CAP, model_width)
    w_gate = expert_gate[0]
    w_up = expert_up[0]
    w_down = expert_down[0]
    outgoing = jnp.repeat(packed, group_size, axis=0)
    arrived = lax.all_to_all(outgoing, "exp", split_axis=0, concat_axis=0, tiled=True)
    sources = arrived.shape[0]
    item_count = arrived.shape[1]
    flat_rows = arrived.reshape(sources * item_count, model_width)
    gate_proj = jnp.dot(flat_rows, w_gate, preferred_element_type=jnp.float32)
    up_proj = jnp.dot(flat_rows, w_up, preferred_element_type=jnp.float32)
    hid_rows = (jax.nn.silu(gate_proj) * up_proj).astype(jnp.bfloat16)
    partial_value = jnp.dot(hid_rows, w_down, preferred_element_type=jnp.float32).astype(
        jnp.bfloat16
    )
    partial_value = partial_value.reshape(sources, item_count, model_width)
    returned = lax.all_to_all(partial_value, "exp", split_axis=0, concat_axis=0, tiled=True)
    expert_out = jnp.sum(
        returned.reshape(EXPERTS, group_size, CAP, model_width).astype(jnp.float32), axis=1
    )
    expert_out = expert_out.astype(jnp.bfloat16).reshape(EXPERTS * CAP, model_width)
    b_sum = jnp.dot(mixing, expert_out.astype(jnp.float32), precision=lax.Precision.HIGHEST)
    b_out = (b_float + b_sum).astype(jnp.bfloat16)
    return (a_out, b_out)


def solution(mesh):
    return jax.shard_map(
        shards,
        mesh=mesh,
        in_specs=(
            P(("rep", "exp"), None),
            P(),
            P(None, "exp"),
            P(None, "exp"),
            P("exp", None),
            P(("rep", "exp"), None),
            P(),
            P(("rep", "exp"), None),
            P(("rep", "exp"), None),
            P("exp", None, None),
            P("exp", None, None),
            P("exp", None, None),
        ),
        out_specs=(P(("rep", "exp"), None), P(("rep", "exp"), None)),
        check_vma=False,
    )
```

profile of v0, /device:TPU:0, one launch (start us, length us, event | category | flops | bytes accessed | tf_op | source)
XLA Modules:
  0.0 187.6 jit_solution(7386849695847131397)
XLA Ops:
  7.2 0.0 copy-start
  7.2 1.0 fusion.32
  8.2 0.8 convert_reduce_fusion
  9.0 0.1 eq.45
  9.1 0.1 mul.80
  9.2 0.1 mul.83
  9.3 0.1 eq.40
  9.4 0.1 eq.43
  9.5 1.2 convolution_convert_fusion
  10.7 1.2 reshape_broadcast_in_dim_reshape.3
  11.9 7.4 %all-to-all-start = ((bf16[16,3,7168]{2,1,0:T(4,128)(2,1)}), bf16[16,3,7168]{2,1,0:T(4,128)(2,1)S(1)}, u32[]{:S(2)}, u32[]{:S(2)}) async-start(bf16[16,3,7168]{2,1,0:T(4,128)(2,1)} %reshape_broadcast_in_dim_reshape.3), calls=%async_computation | async-start | bytes 1835008 | tf_op jit(solution)/shard_map/all_to_all | solution.py:65
  19.3 0.0 all-reduce.3.cloned.1.call-start
  19.4 0.9 fusion.37
  20.3 0.9 fusion.44
  21.2 31.0 %all-gather = bf16[16,2,7168]{2,1,0:T(2,128)(2,1)S(1)} all-gather(bf16[1,2,7168]{2,1,0:T(2,128)(2,1)S(1)} %fusion.44), channel_id=1, replica_groups=mesh['rep'=2,'exp'=16] {'exp'}, dimensions={0}, use_global_device_ids=true | all-gather | bytes 487424 | tf_op jit(solution)/shard_map/all_gather | solution.py:33
  52.2 0.2 reshape.53
  52.4 8.5 %fusion.52 = f32[32,1152]{1,0:T(8,128)S(1)} fusion(bf16[32,7168]{1,0:T(8,128)(2,1)S(1)} %reshape.53, bf16[7168,1152]{1,0:T(8,128)(2,1)} %param.14), kind=kOutput, calls=%fused_computation.58 | convolution fusion | flops 528482304 | bytes 17121280 | tf_op jit(solution)/shard_map/dot_general | solution.py:34
  60.8 0.0 copy-start.3
  60.8 0.0 copy-start.4
  60.8 17.0 %fusion.21 = f32[32,7168]{1,0:T(8,128)} fusion(bf16[1152,7168]{1,0:T(8,128)(2,1)} %param.16, bf16[32,7168]{1,0:T(8,128)(2,1)S(1)} %reshape.53, bf16[7168,1152]{1,0:T(8,128)(2,1)} %param.15, f32[32,1152]{1,0:T(8,128)S(1)} %fusion.52), kind=kOutput, calls=%fused_computation.16 | convolution fusion | flops 1057185792 | bytes 34553856 | tf_op jit(solution)/shard_map/dot_general | solution.py:39
  77.9 0.0 all-reduce.3.cloned.1.call-update
  77.9 0.0 copy-done
  77.9 0.0 copy-done.3
  77.9 0.2 fusion.45
  78.1 0.1 select_multiply_fusion
  78.2 0.1 copy.19
  78.3 0.0 copy-done.4
  78.3 0.6 dynamic-slice
  79.5 0.0 all-to-all-done
  79.5 0.8 reshape.50
  80.4 8.0 %fusion.4 = f32[48,1024]{1,0:T(8,128)S(1)} fusion(bf16[48,7168]{1,0:T(8,128)(2,1)S(1)} %reshape.50, bf16[1,7168,1024]{2,1,0:T(8,128)(2,1)} %param.21), kind=kOutput, calls=%fused_computation.4 | convolution fusion | flops 704643072 | bytes 15564800 | tf_op jit(solution)/shard_map/dot_general | solution.py:69
  88.4 0.0 copy-start.1
  88.4 0.0 copy-start.2
  88.4 14.8 %fusion.6 = bf16[48,7168]{1,0:T(8,128)(2,1)S(1)} fusion(bf16[1,1024,7168]{2,1,0:T(8,128)(2,1)} %param.23, bf16[48,7168]{1,0:T(8,128)(2,1)S(1)} %reshape.50, bf16[1,7168,1024]{2,1,0:T(8,128)(2,1)} %param.22, f32[48,1024]{1,0:T(8,128)S(1)} %fusion.4), kind=kOutput, calls=%fused_computation.6 | convolution fusion | flops 1409925120 | bytes 30932992 | tf_op jit(solution)/shard_map/dot_general | solution.py:72
  103.2 1.2 reshape.51
  104.4 5.4 %all-to-all-start.1 = ((bf16[16,3,7168]{2,1,0:T(4,128)(2,1)}), bf16[16,3,7168]{2,1,0:T(4,128)(2,1)S(1)}, u32[]{:S(2)}, u32[]{:S(2)}) async-start(bf16[16,3,7168]{2,1,0:T(4,128)(2,1)} %reshape.51), calls=%async_computation.1 | async-start | bytes 1835008 | tf_op jit(solution)/shard_map/all_to_all | solution.py:76
  109.8 68.1 %all-reduce.3.cloned.1.call-done = f32[32,7168]{1,0:T(8,128)} async-done(((f32[32,7168]{1,0:T(8,128)}), f32[32,7168]{1,0:T(8,128)}) %all-reduce.3.cloned.1.call-update) | async-done | bytes 917520
  177.9 0.0 copy-done.1
  177.9 1.6 fusion.40
  179.5 0.0 all-to-all-done.1
  179.5 0.0 copy-done.2
  179.5 1.2 fusion.10
  (5 shorter events, 0.1 us)
Async XLA Ops:
  7.2 70.7 %copy-start = (f32[4,8]{1,0:T(4,128)S(1)}, f32[4,8]{1,0:T(4,128)}, u32[]{:S(2)}) copy-start(f32[4,8]{1,0:T(4,128)} %param.20) | copy-start | bytes 388
  11.9 67.6 %all-to-all-start = ((bf16[16,3,7168]{2,1,0:T(4,128)(2,1)}), bf16[16,3,7168]{2,1,0:T(4,128)(2,1)S(1)}, u32[]{:S(2)}, u32[]{:S(2)}) async-start(bf16[16,3,7168]{2,1,0:T(4,128)(2,1)} %reshape_broadcast_in_dim_reshape.3), calls=%async_computation | async-start | bytes 1835008 | tf_op jit(solution)/shard_map/all_to_all | solution.py:65
  19.3 158.6 %all-reduce.3.cloned.1.call-start = ((), (), s32[]{:S(2)}) async-start(), calls=%async_computation.2 | async-start | bytes 1835008
  60.8 17.1 %copy-start.3 = (s32[4,8]{1,0:T(4,128)S(1)}, s32[4,8]{1,0:T(4,128)}, u32[]{:S(2)}) copy-start(s32[4,8]{1,0:T(4,128)} %param.19) | copy-start | bytes 388
  60.8 17.5 %copy-start.4 = (u32[32]{0:T(128)S(1)}, u32[32]{0:T(128)}, u32[]{:S(2)}) copy-start(u32[32]{0:T(128)} %constant.28) | copy-start | bytes 388
  88.4 89.5 %copy-start.1 = (bf16[2,7168]{1,0:T(2,128)(2,1)S(1)}, bf16[2,7168]{1,0:T(2,128)(2,1)}, u32[]{:S(2)}) copy-start(bf16[2,7168]{1,0:T(2,128)(2,1)} %param.12) | copy-start | bytes 86020
  88.4 91.1 %copy-start.2 = (bf16[4,7168]{1,0:T(4,128)(2,1)S(1)}, bf16[4,7168]{1,0:T(4,128)(2,1)}, u32[]{:S(2)}) copy-start(bf16[4,7168]{1,0:T(4,128)(2,1)} %param.17) | copy-start | bytes 172036
  104.4 75.1 %all-to-all-start.1 = ((bf16[16,3,7168]{2,1,0:T(4,128)(2,1)}), bf16[16,3,7168]{2,1,0:T(4,128)(2,1)S(1)}, u32[]{:S(2)}, u32[]{:S(2)}) async-start(bf16[16,3,7168]{2,1,0:T(4,128)(2,1)} %reshape.51), calls=%async_computation.1 | async-start | bytes 1835008 | tf_op jit(solution)/shard_map/all_to_all | solution.py:76
Sparse Core Ops, SparseCore 0:
  78.0 99.8 all-reduce.2
where the time goes:
time: 188 us
  waiting for transfers between devices  68.1 us (36%)
  matrix products  50.9 us (27%)
  blocking collectives  31 us (16%)
  between operations  14.8 us (8%)
  starting transfers between devices  12.9 us (7%)
  other arithmetic  5.3 us (3%)
  local copies, waits for them, and re-layouts  4.55 us (2%)
    unnamed x2, waiting for transfers between devices  68.1 us
    all_gather x1, blocking collectives, shards(): block_rows = lax.all_gather(a_normed, 'exp', axis=0, tiled=True)  31 us
    dot_general x1, matrix products, shards(): jnp.dot(block_rows, dense_down, preferred_element_type=jnp.float32)  17 us
    dot_general x1, matrix products, shards(): jnp.dot(hid_rows, w_down, preferred_element_type=jnp.float32)  14.8 us
    dot_general x1, matrix products, shards(): jnp.dot(block_rows, dense_gate, preferred_element_type=jnp.float32)  8.46 us
    dot_general x1, matrix products, shards(): gate_proj = jnp.dot(flat_rows, w_gate, preferred_element_type=jnp.float32)  7.99 us
    all_to_all x1, starting transfers between devices, shards(): lax.all_to_all(outgoing, 'exp', split_axis=0, concat_axis=0, tiled=True)  7.41 us
    all_to_all x1, starting transfers between devices, shards(): lax.all_to_all(partial_value, 'exp', split_axis=0, concat_axis=0, tiled=T...  5.4 us
  transfers between devices with their start and end apart: 3, of which 1 were waited for; matrix products, arithmetic and copies ran while one was open for 29% of the time, Pallas kernels for 0%

commit v1 on v0

v1 whole, which is shorter than its diff:
```python
import functools

import jax
import jax.numpy as jnp
from jax import lax
from jax.experimental import pallas as pl
from jax.experimental.pallas import tpu as pltpu
from jax.sharding import PartitionSpec as P

EXPERTS = 16
LANES = 128
EARLY = 6
LAG = 2
F32 = jnp.float32
BF16 = jnp.bfloat16


def pick(total, sizes):
    for size in sizes:
        if total % size == 0:
            return size
    return total


def normed(values, gain_row):
    mean = jnp.mean(values * values, axis=-1, keepdims=True)
    return values * lax.rsqrt(mean + 1e-06) * gain_row


def kernel(
    n, kc, cn,
    a_ref, ag_ref, b_ref, bg_ref, ids_ref, rw_ref,
    dg_hbm, du_hbm, dd_hbm, eg_hbm, eu_hbm, ed_hbm,
    a_out, b_out,
    gu, dn, gat_b, gat_a, g_acc, u_acc, hid_b, hid_a,
    mine_b, s1_b, r1_b, s2_b, r2_b,
    mine_a, s1_a, r1_a, s2_a, r2_a,
    gu_sem, dn_sem, gat_send, gat_recv, fwd_send, fwd_recv,
    s1_send, s1_recv, s2_send, s2_recv,
):
    me = lax.axis_index("exp")
    core = lax.rem(me, 2)
    chip = me // 2
    chips = n // 2
    sibling = chip * 2 + (1 - core)
    expert = me // (n // EXPERTS)
    width = a_ref.shape[1]
    steps = width // kc
    groups = width // cn
    es = eg_hbm.shape[2]
    fd = dg_hbm.shape[1]
    wide = gu.shape[3]
    tall = dn.shape[1]

    def peer(offset):
        return lax.rem(chip + offset + chips, chips) * 2 + core

    def cols(j, size):
        return pl.ds(pl.multiple_of(j * size, size), size)

    def slot_gu(which, k, used):
        return gu.at[which, k] if used == wide else gu.at[which, k, :, pl.ds(0, used)]

    def slot_dn(j, used):
        return dn.at[j] if used == tall else dn.at[j, pl.ds(0, used), :]

    def e_gu(which, k):
        src = (eg_hbm, eu_hbm)[which].at[0, cols(k, kc), :]
        return pltpu.make_async_copy(src, slot_gu(which, k, es), gu_sem.at[which, k])

    def d_gu(which, k):
        src = (dg_hbm, du_hbm)[which].at[cols(k, kc), :]
        return pltpu.make_async_copy(src, slot_gu(which, k, fd), gu_sem.at[which, k])

    def e_dn(j):
        return pltpu.make_async_copy(ed_hbm.at[0, :, cols(j, cn)], slot_dn(j, es), dn_sem.at[j])

    def d_dn(j):
        return pltpu.make_async_copy(dd_hbm.at[:, cols(j, cn)], slot_dn(j, fd), dn_sem.at[j])

    def start_gu(k, carry):
        e_gu(0, k).start()
        e_gu(1, k).start()
        return carry

    def start_dn(j, carry):
        e_dn(j).start()
        return carry

    barrier = pltpu.get_barrier_semaphore()

    def greet(o, carry):
        pl.semaphore_signal(
            barrier, inc=1, device_id={"exp": peer(o)}, device_id_type=pl.DeviceIdType.MESH
        )
        return carry

    lax.fori_loop(1, chips, greet, 0)
    pl.semaphore_signal(
        barrier, inc=1, device_id={"exp": sibling}, device_id_type=pl.DeviceIdType.MESH
    )
    early = min(EARLY, steps)
    lax.fori_loop(0, early, start_gu, 0)

    rows_b = b_ref.shape[0]
    gat_b[0, core, :, pl.ds(0, width)] = normed(b_ref[...].astype(F32), bg_ref[...]).astype(BF16)
    lane = lax.broadcasted_iota(jnp.int32, (rows_b, LANES), 1)
    table = jnp.zeros((rows_b, LANES), F32)
    for k in range(ids_ref.shape[1]):
        table = table + jnp.where(ids_ref[:, k : k + 1] == lane, rw_ref[:, k : k + 1], 0.0)
    high = table.astype(BF16)
    gat_b[0, core, :, pl.ds(width, LANES)] = high
    gat_b[0, core, :, pl.ds(width + LANES, LANES)] = (table - high.astype(F32)).astype(BF16)
    gat_a[0, core] = normed(a_ref[...].astype(F32), ag_ref[...]).astype(BF16)

    pl.semaphore_wait(barrier, chips)

    def remote(src, dst, send, recv, target):
        return pltpu.make_async_remote_copy(
            src_ref=src, dst_ref=dst, send_sem=send, recv_sem=recv,
            device_id={"exp": target}, device_id_type=pl.DeviceIdType.MESH,
        )

    def gather_copy(ph, o):
        buf = (gat_b, gat_a)[ph]
        return remote(
            buf.at[0, core], buf.at[o, core], gat_send.at[ph], gat_recv.at[ph, o], peer(o)
        )

    def forward_copy(ph, o):
        buf = (gat_b, gat_a)[ph]
        return remote(
            buf.at[o, core], buf.at[o, core], fwd_send.at[ph], fwd_recv.at[ph], sibling
        )

    def gather_start(ph):
        def go(o, carry):
            gather_copy(ph, o).start()
            return carry

        lax.fori_loop(1, chips, go, 0)
        forward_copy(ph, 0).start()

    def gather_forward(ph):
        def go(o, carry):
            gather_copy(ph, o).wait_recv()
            forward_copy(ph, o).start()
            return carry

        lax.fori_loop(1, chips, go, 0)

    def gather_finish(ph):
        buf = (gat_b, gat_a)[ph]
        block = buf.at[:, 1 - core]
        pltpu.make_async_copy(block, block, fwd_recv.at[ph]).wait()

    gather_start(0)
    gather_start(1)
    lax.fori_loop(early, steps, start_gu, 0)
    lax.fori_loop(0, groups, start_dn, 0)
    gather_forward(0)
    gather_finish(0)

    def rows_of(buf, where):
        pieces = [buf[o, c, :, where].astype(F32) for c in range(2) for o in range(chips)]
        return jnp.concatenate(pieces, axis=0)

    def hidden(ph, used, copy, after, buf, out):
        total = buf.shape[0] * 2 * buf.shape[2]
        ga = g_acc.at[pl.ds(0, total), pl.ds(0, used)]
        ua = u_acc.at[pl.ds(0, total), pl.ds(0, used)]
        ga[...] = jnp.zeros(ga.shape, F32)
        ua[...] = jnp.zeros(ua.shape, F32)

        def step(k, carry):
            x = rows_of(buf, cols(k, kc)).astype(BF16)
            copy(0, k).wait()
            ga[...] += jnp.dot(x, slot_gu(0, k, used)[...], preferred_element_type=F32)
            copy(1, k).wait()
            ua[...] += jnp.dot(x, slot_gu(1, k, used)[...], preferred_element_type=F32)
            after(k)
            return carry

        lax.fori_loop(0, steps, step, 0)
        g = ga[...]
        out[...] = (g / (1.0 + jnp.exp(-g)) * ua[...]).astype(BF16)

    def pair_copy(ph, j):
        src, dst = ((s1_b, r1_b), (s1_a, r1_a))[ph]
        return remote(
            src.at[:, cols(j, cn)], dst.at[:, cols(j, cn)],
            s1_send.at[ph], s1_recv.at[ph, j], sibling,
        )

    def down(ph, used, copy, after, hid, scale):
        mine, s1, r1, s2, r2 = (
            (mine_b, s1_b, r1_b, s2_b, r2_b), (mine_a, s1_a, r1_a, s2_a, r2_a)
        )[ph]
        half = mine.shape[0]
        rows = half // chips

        def finish(j):
            where = cols(j, cn)
            pair_copy(ph, j).wait_recv()
            both = mine[:, where] + r1[:, where].astype(F32)
            mine[:, where] = both
            for o in range(1, chips):
                s2[o - 1, :, where] = both[o * rows : (o + 1) * rows].astype(BF16)

            def send(o, carry):
                remote(
                    s2.at[o - 1, :, where], r2.at[o - 1, :, where],
                    s2_send.at[ph], s2_recv.at[ph], peer(-o),
                ).start()
                return carry

            lax.fori_loop(1, chips, send, 0)

        def step(j, carry):
            where = cols(j, cn)
            copy(j).wait()
            part = jnp.dot(hid[...], slot_dn(j, used)[...], preferred_element_type=F32)
            if scale is not None:
                part = part * scale
            first, second = part[:half], part[half:]
            mine[:, where] = jnp.where(core == 0, first, second)
            s1[:, where] = jnp.where(core == 0, second, first).astype(BF16)
            pair_copy(ph, j).start()
            after(j)

            @pl.when(j >= LAG)
            def _():
                finish(j - LAG)

            return carry

        lax.fori_loop(0, groups, step, 0)

        def rest(j, carry):
            finish(j)
            return carry

        lax.fori_loop(max(groups - LAG, 0), groups, rest, 0)

    def result(ph, own, out):
        mine, r2 = ((mine_b, r2_b), (mine_a, r2_a))[ph]
        pltpu.make_async_copy(r2, r2, s2_recv.at[ph]).wait()
        rows = out.shape[0]

        def step(j, carry):
            where = cols(j, cn)
            total = mine[pl.ds(0, rows), where]
            for o in range(chips - 1):
                total = total + r2[o, :, where].astype(F32)
            out[:, where] = (own[:, where].astype(F32) + total).astype(BF16)
            return carry

        lax.fori_loop(0, groups, step, 0)

    def next_gu(k):
        d_gu(0, k).start()
        d_gu(1, k).start()

    def nothing(k):
        return None

    hidden(0, es, e_gu, next_gu, gat_b, hid_b)
    gather_forward(1)
    tables = rows_of(gat_b, pl.ds(width, LANES)) + rows_of(gat_b, pl.ds(width + LANES, LANES))
    chosen = lax.broadcasted_iota(jnp.int32, tables.shape, 1) == expert
    scale = jnp.sum(jnp.where(chosen, tables, 0.0), axis=1, keepdims=True)
    down(0, es, e_dn, lambda j: d_dn(j).start(), hid_b, scale)
    gather_finish(1)
    hidden(1, fd, d_gu, nothing, gat_a, hid_a)
    down(1, fd, d_dn, nothing, hid_a, None)
    result(0, b_ref, b_out)
    result(1, a_ref, a_out)

    for ph in range(2):
        buf = (gat_b, gat_a)[ph]
        s1, s2 = ((s1_b, s2_b), (s1_a, s2_a))[ph]
        sent = buf.at[pl.ds(0, chips - 1), 0]
        pltpu.make_async_copy(sent, sent, gat_send.at[ph]).wait()
        sent = buf.at[:, 0]
        pltpu.make_async_copy(sent, sent, fwd_send.at[ph]).wait()
        pltpu.make_async_copy(s1, s1, s1_send.at[ph]).wait()
        pltpu.make_async_copy(s2, s2, s2_send.at[ph]).wait()


def shards(
    a_tokens, a_gain, dense_gate, dense_up, dense_down, b_tokens, b_gain, expert_ids,
    route_weights, expert_gate, expert_up, expert_down,
):
    n = lax.axis_size("exp")
    chips = n // 2
    ra, width = a_tokens.shape
    rb = b_tokens.shape[0]
    fd = dense_gate.shape[1]
    es = expert_gate.shape[2]
    wide = max(fd, es)
    kc = pick(width, (512, 256, 128))
    cn = pick(width, (1024, 512, 256, 128))
    steps, groups = width // kc, width // cn
    extra = width + 2 * LANES
    most = n * max(ra, rb)

    def back(rows):
        return [
            pltpu.VMEM((chips * rows, width), F32),
            pltpu.VMEM((chips * rows, width), BF16),
            pltpu.VMEM((chips * rows, width), BF16),
            pltpu.VMEM((chips - 1, rows, width), BF16),
            pltpu.VMEM((chips - 1, rows, width), BF16),
        ]

    vmem = pl.BlockSpec(memory_space=pltpu.VMEM)
    hbm = pl.BlockSpec(memory_space=pl.ANY)
    dma = pltpu.SemaphoreType.DMA
    weights = 3 * width * (fd + es)
    return pl.pallas_call(
        functools.partial(kernel, n, kc, cn),
        out_shape=(
            jax.ShapeDtypeStruct(a_tokens.shape, BF16),
            jax.ShapeDtypeStruct(b_tokens.shape, BF16),
        ),
        in_specs=[vmem] * 6 + [hbm] * 6,
        out_specs=(vmem, vmem),
        scratch_shapes=[
            pltpu.VMEM((2, steps, kc, wide), BF16),
            pltpu.VMEM((groups, wide, cn), BF16),
            pltpu.VMEM((chips, 2, rb, extra), BF16),
            pltpu.VMEM((chips, 2, ra, width), BF16),
            pltpu.VMEM((most, wide), F32),
            pltpu.VMEM((most, wide), F32),
            pltpu.VMEM((n * rb, es), BF16),
            pltpu.VMEM((n * ra, fd), BF16),
            *back(rb),
            *back(ra),
            dma((2, steps)),
            dma((groups,)),
            dma((2,)),
            dma((2, chips)),
            dma((2,)),
            dma((2,)),
            dma((2,)),
            dma((2, groups)),
            dma((2,)),
            dma((2,)),
        ],
        compiler_params=pltpu.CompilerParams(
            collective_id=0, has_side_effects=True, vmem_limit_bytes=67043328
        ),
        cost_estimate=pl.CostEstimate(
            flops=2 * n * max(ra, rb) * weights, bytes_accessed=2 * weights, transcendentals=0
        ),
    )(
        a_tokens, a_gain.reshape(1, width), b_tokens, b_gain.reshape(1, width),
        expert_ids, route_weights,
        dense_gate, dense_up, dense_down, expert_gate, expert_up, expert_down,
    )


def solution(mesh):
    return jax.shard_map(
        shards,
        mesh=mesh,
        in_specs=(
            P(("rep", "exp"), None),
            P(),
            P(None, "exp"),
            P(None, "exp"),
            P("exp", None),
            P(("rep", "exp"), None),
            P(),
            P(("rep", "exp"), None),
            P(("rep", "exp"), None),
            P("exp", None, None),
            P("exp", None, None),
            P("exp", None, None),
        ),
        out_specs=(P(("rep", "exp"), None), P(("rep", "exp"), None)),
        check_vma=False,
    )
```

time: 188 us -> 61.7 us (0.33)
  waiting for transfers between devices: 68.1 us -> 0 us
  Pallas kernels: 0 us -> 57.9 us
  matrix products: 50.9 us -> 0 us
  blocking collectives: 31 us -> 0 us
  between operations: 14.8 us -> 0.64 us
  starting transfers between devices: 12.9 us -> 0 us
  other arithmetic: 5.3 us -> 0 us
    unnamed x2 -> x0, waiting for transfers between devices: 68.1 us -> none
    pallas_call x0 -> x1, Pallas kernels: none -> 57.9 us  [shards(): pl.pallas_call(functools.partial(kernel, n, kc, cn), out_shape=(jax.Shape...]
    dot_general x7 -> x0, matrix products: 50.9 us -> none  [the longest x1 17 us: shards(): jnp.dot(block_rows, dense_down, preferred_element_type=jnp.float32)]
    all_gather x1 -> x0, blocking collectives: 31 us -> none  [shards(): block_rows = lax.all_gather(a_normed, 'exp', axis=0, tiled=True)]
    all_to_all x2 -> x0, starting transfers between devices: 12.8 us -> none  [the longest x1 7.41 us: shards(): lax.all_to_all(outgoing, 'exp', split_axis=0, concat_axis=0, tiled=True)]
    reduce_sum x3 -> x0, other arithmetic: 2.69 us -> none  [the longest x2 1.92 us: normed(): jnp.mean(values * values, axis=-1, keepdims=True) + 1e-06]
    unnamed x12 -> x2, local copies, waits for them, and re-layouts: 0.8 us -> 2.84 us
    reshape x2 -> x0, local copies, waits for them, and re-layouts: 2.01 us -> none  [the longest x1 1.21 us: shards(): partial_value = partial_value.reshape(sources, item_count, model_width)]
  transfers between devices with their start and end apart: 3 -> 0, of which waited for: 1 -> 0; matrix products, arithmetic and copies ran while one was open for 29% -> 0% of each run, Pallas kernels for 0% -> 0%
where the time goes in v1:
time: 61.7 us; the launch traced here: 61.4 us
  Pallas kernels  57.9 us (94%)
  local copies, waits for them, and re-layouts  2.84 us (5%)
  between operations  0.64 us (1%)
    pallas_call x1, Pallas kernels, shards(): pl.pallas_call(functools.partial(kernel, n, kc, cn), out_shape=(jax.Shape...  57.9 us
    unnamed x2, local copies, waits for them, and re-layouts  2.84 us

profile of v1, /device:TPU:0, one launch (start us, length us, event | category | flops | bytes accessed | tf_op | source)
XLA Modules:
  0.0 61.4 jit_solution(18105292014409353149)
XLA Ops:
  0.6 57.9 %shard_map.131 = (bf16[2,7168]{1,0:T(2,128)(2,1)}, bf16[4,7168]{1,0:T(4,128)(2,1)}) custom-call(bf16[2,7168]{1,0:T(2,128)(2,1)} %a_ref.1, f32[1,7168]{1,0:T(1,128)} %bitcast.2, bf16[4,7168]{1,0:T(4,128)(2,1)} %b_ref.1, f32[1,7168]{1,0:T(1,128)} %bitcast.3, s32[4,8]{1,0:T(4,128)} %ids_ref.1, f32[4,8]{1,0:T(4,128)} %rw_ref.1, bf16[7168,1152]{1,0:T(8,128)(2,1)} %dg_hbm.1, ...), custom_call_target="tpu_custom_call" | custom-call | flops 5989466112 | bytes 93585408 | tf_op jit(solution)/shard_map/pallas_call | solution.py:320
  58.5 1.4 %copy.16 = bf16[2,7168]{1,0:T(2,128)(2,1)} copy(bf16[2,7168]{1,0:T(2,128)(2,1)} %get-tuple-element.4) | data formatting | bytes 57344
  59.9 1.5 %copy.17 = bf16[4,7168]{1,0:T(4,128)(2,1)} copy(bf16[4,7168]{1,0:T(4,128)(2,1)} %get-tuple-element.5) | data formatting | bytes 114688
